TPU v7x, 128 devices: a whole 4x4x4 slice. The times are simulated.
128 devices in a mesh: fsdp: 32 (over z, x, core), tp: 4 (over y).
Axes of the slice: x: 4, y: 4, z: 4, core: 2. Of those that a mesh axis runs over, the one named last changes fastest.
Arguments:
- gradients: bfloat16 [2, 8192, 8192], P(None, 'fsdp', 'tp'), may hold values from -120 to 120
- row_counts: int32 [32], replicated, may hold values from 128 to 256, as said below
- block_owner: int32 [2, 8], replicated, may hold values from 0 to 31, as said below
Outputs:
- update: bfloat16 [2, 8192, 8192], P(None, 'fsdp', 'tp')
- owned: bfloat16 [32768, 4096], P('fsdp', 'tp')
Inputs may be any that keep to these rules, and one draw needn't show every extreme that they name: `row_counts`: every count is a multiple of 128; some index holds exactly 256. `block_owner`: blocks whose columns lie on the same tp index have distinct owners.
All inputs are finite; a program needn't handle non-finite values.
Results may differ from a plain program's by a relative error of at most 0.005.
The roundings to bfloat16 on the way count: a program that leaves them out, or rounds other values in their place, can miss the bound.
Values may be sent and summed in bfloat16 or wider, within the bound.
No kernel may reach another device: no remote copies, remote signals or barrier semaphores. Data moves between devices by JAX's collectives and lax.ppermute only.
A program may use at most 128 MiB of HBM per device.

v0:
```python
import jax
import jax.numpy as jnp
from jax import lax
from jax.sharding import PartitionSpec as P

BLOCK = 1024


damping = 0.01


def broadcast(block, axis, owner):
    block = jnp.where(lax.axis_index(axis) == owner, block, jnp.zeros_like(block))
    return lax.psum(block, axis)


def newton_root(statistic):
    identity = jnp.eye(statistic.shape[0], dtype=jnp.float32)
    scaling = 2.5 / jnp.sqrt(jnp.sum(statistic * statistic))
    scaled = scaling * statistic
    factor_one = (5.0 * identity - scaled) / 4.0
    square = jnp.dot(factor_one, factor_one, precision=lax.Precision.HIGHEST)
    inner_part = jnp.dot(square, scaled, precision=lax.Precision.HIGHEST)
    contracted = jnp.dot(square, inner_part, precision=lax.Precision.HIGHEST)
    factor_two = (5.0 * identity - contracted) / 4.0
    result = jnp.dot(
        jnp.sqrt(jnp.sqrt(scaling)) * factor_one, factor_two, precision=lax.Precision.HIGHEST
    )
    return result.astype(jnp.bfloat16)


def blank_root(statistic):
    return jnp.zeros(statistic.shape, jnp.bfloat16)


def body(gradients, row_counts, block_owner):
    fsdp_index = lax.axis_index("fsdp")
    tp_index = lax.axis_index("tp")
    layers, row_slots, columns = gradients.shape
    per_device = columns // BLOCK
    block_total = layers * per_device
    limit = row_counts[fsdp_index]
    valid_rows = (jnp.arange(row_slots, dtype=jnp.int32) < limit).astype(jnp.bfloat16)
    blocked = (gradients * valid_rows[None, :, None]).reshape(layers, row_slots, per_device, BLOCK)
    partial_value = jnp.einsum(
        "lrkb,lrke->lkbe", blocked, blocked, preferred_element_type=jnp.float32
    )
    partial_value = partial_value.reshape(block_total, BLOCK, BLOCK)
    identity = jnp.eye(BLOCK, dtype=jnp.float32)
    total_rows = jnp.sum(row_counts).astype(jnp.float32)
    local_owner = lax.dynamic_slice(
        block_owner, (jnp.int32(0), tp_index * per_device), (layers, per_device)
    )
    local_owner = local_owner.reshape(block_total)
    owned_mask = local_owner == fsdp_index
    summed = lax.psum(partial_value, "fsdp")
    statistic = summed / total_rows + damping * identity
    chosen = jnp.sum(jnp.where(owned_mask[:, None, None], statistic, 0.0), axis=0)
    owned_root = lax.cond(jnp.any(owned_mask), newton_root, blank_root, chosen)
    received = []
    for position in range(block_total):
        received.append(broadcast(owned_root, "fsdp", local_owner[position]))
    root_list = jnp.stack(received).reshape(layers, per_device, BLOCK, BLOCK)
    update = jnp.einsum("lrkb,lkbe->lrke", blocked, root_list, preferred_element_type=jnp.float32)
    return (update.astype(jnp.bfloat16).reshape(layers, row_slots, columns), owned_root)


def solution(mesh):
    placed = (P(None, "fsdp", "tp"), P(), P())
    return jax.shard_map(
        body,
        mesh=mesh,
        in_specs=placed,
        out_specs=(P(None, "fsdp", "tp"), P("fsdp", "tp")),
        check_vma=False,
    )
```

profile of v0, /device:TPU:6, one launch (start us, length us, event | category | flops | bytes accessed | tf_op | source)
XLA Modules:
  0.0 442.5 jit_solution(1876236719988741868)
XLA Ops:
  7.2 0.0 all-reduce.4.cloned.1.call-start
  7.2 1.2 dynamic_slice.7
  8.5 0.6 compare_convert_fusion
  9.1 1.8 broadcast_multiply_fusion
  10.9 8.1 %fusion.31 = f32[2,2,1024,1024]{3,2,1,0:T(8,128)} fusion(bf16[2,32,2,8,1024]{4,3,2,1,0:T(8,128)(2,1)S(1)} %bitcast.34), kind=kOutput, calls=%fused_computation.34 | convolution fusion | flops 2147483648 | bytes 18874368 | tf_op jit(solution)/shard_map/lrkb,lrke->lkbe/dot_general | solution.py:45
  19.0 0.0 copy-start.3
  19.0 0.0 copy-start.2
  19.0 0.0 all-reduce.4.cloned.1.call-update
  19.0 0.0 all-reduce.6.cloned.1.call-start
  19.1 0.6 copy-done.3
  19.7 0.6 reduce_sum.36
  20.9 0.0 copy-done.2
  21.0 0.7 compare_reduce_fusion
  22.3 0.1 reshape.36
  22.4 0.7 fusion.38
  25.6 174.8 %all-reduce.4.cloned.1.call-done = f32[4,1024,1024]{2,1,0:T(8,128)} async-done(((f32[4,1024,1024]{2,1,0:T(8,128)}), f32[4,1024,1024]{2,1,0:T(8,128)}) %all-reduce.4.cloned.1.call-update) | async-done | bytes 16777232 | tf_op jit(solution)/shard_map/psum | solution.py:56
  200.4 2.2 iota.36
  202.6 2.5 iota.37
  205.1 88.1 %conditional.1 = (bf16[1024,1024]{1,0:T(8,128)(2,1)}) conditional(s32[]{:T(128)} %convert_element_type.26, () %tuple.23, (s32[]{:T(128)}, s32[2,2]{1,0:T(2,128)S(1)}, f32[]{:T(128)}, f32[4,1024,1024]{2,1,0:T(8,128)}, s32[1,1024,1024]{2,1,0:T(8,128)}, /*index=5*/s32[1,1024,1024]{2,1,0:T(8,128)}) %tuple.24), branch_computations={%region_3.4_spmd, %region_4.7_spmd} | conditional | flops 51576307712 | bytes 119537840 | solution.py:59
  205.1 6.8 %select_bitcast_fusion = f32[1024,1024]{1,0:T(8,128)} fusion(s32[1,1024,1024]{2,1,0:T(8,128)} %get-tuple-element.70, s32[1,1024,1024]{2,1,0:T(8,128)} %get-tuple-element.71), kind=kLoop, calls=%fused_computation.9 | loop fusion | flops 2097152 | bytes 12582912 | tf_op jit(solution)/shard_map/add | solution.py:57
  211.9 0.1 eq.38
  212.0 8.6 %select_reduce_fusion = f32[1024,1024]{1,0:T(8,128)S(1)} fusion(f32[4,1024,1024]{2,1,0:T(8,128)} %get-tuple-element.68, f32[1024,1024]{1,0:T(8,128)} %select_bitcast_fusion, f32[]{:T(128)} %get-tuple-element.69, pred[4]{0:T(512)(128)(4,1)S(1)} %eq.38), kind=kLoop, calls=%fused_computation | loop fusion | flops 15728640 | bytes 25165832 | tf_op jit(solution)/shard_map/reduce_sum | solution.py:58
  220.6 0.0 copy-start
  220.6 2.0 copy-done
  222.6 1.7 multiply_reduce_fusion
  225.0 0.0 copy-start.1
  225.0 19.5 %fusion.3 = f32[1024,1024]{1,0:T(8,128)S(1)} fusion(f32[1024,1024]{1,0:T(8,128)} %copy-done, f32[]{:T(128)S(6)} %div.18), kind=kOutput, calls=%fused_computation.5 | convolution fusion | flops 12890144768 | bytes 8388612 | tf_op jit(solution)/shard_map/cond/branch_1_fun/dot_general | solution.py:22
  244.5 0.0 copy-done.1
  244.5 13.4 %fusion.6 = f32[1024,1024]{1,0:T(8,128)S(1)} fusion(f32[1024,1024]{1,0:T(8,128)S(1)} %fusion.3, f32[1024,1024]{1,0:T(8,128)S(1)} %copy-done.1, f32[]{:T(128)S(6)} %div.18), kind=kOutput, calls=%fused_computation.11 | convolution fusion | flops 12885950464 | bytes 12582916 | tf_op jit(solution)/shard_map/cond/branch_1_fun/dot_general | solution.py:23
  258.0 15.3 %fusion.39 = f32[1024,1024]{1,0:T(8,128)} fusion(f32[1024,1024]{1,0:T(8,128)S(1)} %fusion.3, f32[1024,1024]{1,0:T(8,128)S(1)} %fusion.6), kind=kOutput, calls=%fused_computation.48 | convolution fusion | flops 12884901888 | bytes 12582912 | tf_op jit(solution)/shard_map/cond/branch_1_fun/dot_general | solution.py:24
  273.4 19.5 %fusion.18 = bf16[1024,1024]{1,0:T(8,128)(2,1)} fusion(f32[1024,1024]{1,0:T(8,128)} %fusion.39, f32[1024,1024]{1,0:T(8,128)} %copy-done, f32[]{:T(128)S(6)} %mul.41, f32[]{:T(128)S(6)} %div.18), kind=kOutput, calls=%fused_computation.23 | convolution fusion | flops 12895387648 | bytes 10485768 | tf_op jit(solution)/shard_map/cond/branch_1_fun/dot_general | solution.py:26
  293.1 5.1 %select_bitcast_fusion.4 = (bf16[1,1024,1024]{2,1,0:T(8,128)(2,1)}, bf16[1,1024,1024]{2,1,0:T(8,128)(2,1)}, bf16[1,1024,1024]{2,1,0:T(8,128)(2,1)}, bf16[1,1024,1024]{2,1,0:T(8,128)(2,1)}) fusion(bf16[1024,1024]{1,0:T(8,128)(2,1)} %get-tuple-element.96, pred[]{:T(512)S(6)} %eq.47, pred[]{:T(512)S(6)} %eq.52, pred[]{:T(512)S(6)} %eq.51, pred[]{:T(512)S(6)} %eq.50), kind=kLoop, calls=%fused_computation.39 | loop fusion | flops 4194304 | bytes 10485764 | tf_op jit(solution)/shard_map/stack | solution.py:63
  298.2 0.0 all-reduce.6.cloned.1.call-update
  298.2 118.4 %all-reduce.6.cloned.1.call-done = (bf16[1,1024,1024]{2,1,0:T(8,128)(2,1)}, bf16[1,1024,1024]{2,1,0:T(8,128)(2,1)}, bf16[1,1024,1024]{2,1,0:T(8,128)(2,1)}, bf16[1,1024,1024]{2,1,0:T(8,128)(2,1)}) async-done(((bf16[1,1024,1024]{2,1,0:T(8,128)(2,1)}, bf16[1,1024,1024]{2,1,0:T(8,128)(2,1)}, bf16[1,1024,1024]{2,1,0:T(8,128)(2,1)}, bf16[1,1024,1024]{2,1,0:T(8,128)(2,1)}), (bf16[1,1024,1024]{2,1,0:T(8,128)(2,1)}, ...) | async-done | bytes 8388624 | tf_op jit(solution)/shard_map/psum | solution.py:14
  416.6 7.1 %pad_maximum_fusion = bf16[4,1024,1024]{2,1,0:T(8,128)(2,1)} fusion(bf16[1,1024,1024]{2,1,0:T(8,128)(2,1)} %get-tuple-element.78, bf16[1,1024,1024]{2,1,0:T(8,128)(2,1)} %get-tuple-element.79, bf16[1,1024,1024]{2,1,0:T(8,128)(2,1)} %get-tuple-element.80, bf16[1,1024,1024]{2,1,0:T(8,128)(2,1)} %get-tuple-element.81), kind=kLoop, calls=%fused_computation.31 | loop fusion | flops 12582912 | bytes 16777216 | tf_op jit(solution)/shard_map/stack | solution.py:63
  423.7 7.7 %fusion.33 = bf16[2,2,1024,256]{3,2,1,0:T(8,128)(2,1)} fusion(bf16[2,2,1024,1024]{3,2,1,0:T(8,128)(2,1)} %bitcast.36, bf16[2,32,2,8,1024]{4,3,2,1,0:T(8,128)(2,1)S(1)} %bitcast.35), kind=kOutput, calls=%fused_computation.40 | convolution fusion | flops 2148532224 | bytes 12582912 | tf_op jit(solution)/shard_map/lrkb,lkbe->lrke/dot_general | solution.py:64
  431.5 3.9 copy.14
  (1 shorter events, 0.0 us)
Async XLA Ops:
  7.2 193.2 %all-reduce.4.cloned.1.call-start = ((), (), s32[]{:S(2)}) async-start(), calls=%async_computation | async-start | bytes 33554432 | tf_op jit(solution)/shard_map/psum | solution.py:56
  19.0 0.7 copy-start.3
  19.0 1.9 copy-start.2
  19.0 397.6 %all-reduce.6.cloned.1.call-start = ((), (), s32[]{:S(2)}) async-start(), calls=%async_computation.1 | async-start | bytes 16777216 | tf_op jit(solution)/shard_map/psum | solution.py:14
  220.6 2.0 copy-start
  225.0 19.5 %copy-start.1 = (f32[1024,1024]{1,0:T(8,128)S(1)}, f32[1024,1024]{1,0:T(8,128)}, u32[]{:S(2)}) copy-start(f32[1024,1024]{1,0:T(8,128)} %copy-done) | copy-start | bytes 12582916 | tf_op jit(solution)/shard_map/cond
Sparse Core Ops, SparseCore 0:
  19.2 181.1 all-reduce.3
  298.3 118.2 all-reduce.5
where the time goes:
time: 446 us; the launch traced here: 442 us
  waiting for transfers between devices  293 us (66%)
  matrix products  83.6 us (19%)
  other arithmetic  33.1 us (7%)
  between operations  18.1 us (4%)
  local copies, waits for them, and re-layouts  13.3 us (3%)
    psum x1, waiting for transfers between devices, body(): summed = lax.psum(partial_value, 'fsdp')  175 us
    psum x1, waiting for transfers between devices, broadcast(): return lax.psum(block, axis)  118 us
    dot_general x1, matrix products, newton_root(): jnp.dot(jnp.sqrt(jnp.sqrt(scaling)) * factor_one, factor_two, precision=l...  19.5 us
    dot_general x1, matrix products, newton_root(): square = jnp.dot(factor_one, factor_one, precision=lax.Precision.HIGHEST)  19.5 us
    dot_general x1, matrix products, newton_root(): contracted = jnp.dot(square, inner_part, precision=lax.Precision.HIGHEST)  15.3 us
    dot_general x1, matrix products, newton_root(): inner_part = jnp.dot(square, scaled, precision=lax.Precision.HIGHEST)  13.4 us
    another operation x2, other arithmetic, body(): root_list = jnp.stack(received).reshape(layers, per_device, BLOCK, BLOCK)  12.2 us
  transfers between devices with their start and end apart: 2, of which 2 were waited for; matrix products, arithmetic and copies ran while one was open for 0% of the time, Pallas kernels for 0%

commit v1 on v0

v1 whole, which is shorter than its diff:
```python
import jax
import jax.numpy as jnp
from jax import lax
from jax.experimental import pallas as pl
from jax.experimental.pallas import tpu as pltpu
from jax.sharding import Mesh, PartitionSpec as P

BLOCK = 1024
TILE = 128
HALF = 64
WIDE = 640
SIDE = 4
damping = 0.01
F32 = jnp.float32
BF16 = jnp.bfloat16
VMEM = pltpu.CompilerParams(vmem_limit_bytes=56 * 1024 * 1024)


def masked_rows(own, other, own_limit, other_limit):
    rows = lax.broadcasted_iota(jnp.int32, own.shape, 0)
    zero = jnp.zeros_like(own)
    return jnp.where(rows < own_limit, own, zero), jnp.where(rows < other_limit, other, zero)


def gram_kernel(scalars, own, other, *refs):
    outs, (wide, gram) = refs[:8], refs[8:]
    z, x = scalars[1], scalars[2]
    rows = own.shape[1]
    own_value, other_value = masked_rows(own[0], other[...], scalars[3], scalars[4])
    for block in range(2):
        columns = slice(block * BLOCK, (block + 1) * BLOCK)
        wide[:rows, :BLOCK] = own_value[:, columns]
        wide[rows:, :BLOCK] = other_value[:, columns]
        wide[:, BLOCK:] = wide[:, : BLOCK // 2]
        for pair in range(4):
            start = pair * 2 * TILE
            part = lax.dot_general(
                wide[:, start : start + 2 * TILE],
                wide[:, start : start + 6 * TILE],
                (((0,), (0,)), ((), ())),
                preferred_element_type=F32,
            )
            for quarter in range(4):
                shift = TILE * (quarter // 2)
                gram[4 * pair + quarter] = part[
                    quarter * HALF : (quarter + 1) * HALF, shift : shift + WIDE
                ]
        for first in range(SIDE):
            for second in range(SIDE):
                if block == 0:
                    chunk = ((z + second) % SIDE) * SIDE + (x + first) % SIDE
                else:
                    chunk = ((z + first) % SIDE) * SIDE + (x + second) % SIDE
                target = outs[4 * block + first]
                target[second] = gram[chunk].astype(target.dtype)


def first_sum_kernel(*refs):
    ins, outs = refs[:8], refs[8:]
    for side in range(2):
        group = ins[4 * side : 4 * side + 4]
        for second in range(SIDE):
            value = group[0][second]
            for k in range(1, SIDE):
                value = value + group[k][second].astype(F32)
            target = outs[4 * side + second]
            target[...] = value.astype(target.dtype)


def second_sum_kernel(*refs):
    ins, outs = refs[:8], refs[8:]
    for side in range(2):
        group = ins[4 * side : 4 * side + 4]
        value = group[0][...]
        for k in range(1, SIDE):
            value = value + group[k][...].astype(F32)
        outs[side][...] = value.astype(BF16)


def root_kernel(scalars, inverse_rows, own, other, *refs):
    sets, outs, scratch = refs[:8], refs[8:12], refs[12:]
    update_own, update_other, root_own, root_other = outs
    s_ref, w_ref, v_ref, sb_ref, rb_ref, wb_ref = scratch
    block = pl.program_id(0)
    z, x = scalars[1], scalars[2]

    def assemble(group, along_x):
        for first in range(SIDE):
            for second in range(SIDE):
                if along_x:
                    chunk = ((z + second) % SIDE) * SIDE + (x + first) % SIDE
                else:
                    chunk = ((z + first) % SIDE) * SIDE + (x + second) % SIDE
                row = pl.multiple_of(chunk * HALF, HALF)
                slab = chunk // 2
                value = group[first][second].astype(F32)
                for k in range(WIDE // TILE):
                    column = pl.multiple_of(((slab + k) % 8) * TILE, TILE)
                    s_ref[pl.ds(row, HALF), pl.ds(column, TILE)] = value[
                        :, k * TILE : (k + 1) * TILE
                    ]

    @pl.when(block == 0)
    def _():
        assemble(sets[:4], True)
        root_own[...] = jnp.zeros_like(root_own)
        root_other[...] = jnp.zeros_like(root_other)

    @pl.when(block == 1)
    def _():
        assemble(sets[4:], False)

    for slab in range(8):
        for k in range(1, 4):
            far = (slab + k) % 8
            here = slice(slab * TILE, (slab + 1) * TILE)
            there = slice(far * TILE, (far + 1) * TILE)
            s_ref[there, here] = s_ref[here, there].T

    def diagonal(start, rows):
        row = lax.broadcasted_iota(jnp.int32, (rows, BLOCK), 0) + start
        return row == lax.broadcasted_iota(jnp.int32, (rows, BLOCK), 1)

    scale = inverse_rows[0]
    total = jnp.zeros((1, BLOCK), F32)
    for slab in range(8):
        here = slice(slab * TILE, (slab + 1) * TILE)
        value = s_ref[here, :] * scale
        value = value + jnp.where(diagonal(slab * TILE, TILE), damping, 0.0)
        s_ref[here, :] = value
        total = total + jnp.sum(value * value, axis=0, keepdims=True)
    norm = jnp.sum(total, axis=1, keepdims=True)
    scaling = 2.5 / jnp.sqrt(norm)
    for slab in range(8):
        here = slice(slab * TILE, (slab + 1) * TILE)
        value = s_ref[here, :] * scaling
        s_ref[here, :] = value
        sb_ref[here, :] = value.astype(BF16)
    step = 256
    for part in range(BLOCK // step):
        here = slice(part * step, (part + 1) * step)
        square = jnp.dot(sb_ref[here, :], sb_ref[...], preferred_element_type=F32)
        value = s_ref[here, :]
        rb_ref[here, :] = ((10.0 * value - square) * (1.0 / 16.0)).astype(BF16)
        inner = (5.0 * value - square) * 0.25
        w_ref[here, :] = inner
        wb_ref[here, :] = inner.astype(BF16)
    for part in range(BLOCK // step):
        here = slice(part * step, (part + 1) * step)
        product = jnp.dot(rb_ref[here, :], wb_ref[...], preferred_element_type=F32)
        inner = (25.0 / 16.0) * w_ref[here, :] - product
        v_ref[here, :] = inner
        sb_ref[here, :] = inner.astype(BF16)
    quarter = jnp.sqrt(jnp.sqrt(scaling))
    for part in range(BLOCK // step):
        here = slice(part * step, (part + 1) * step)
        product = jnp.dot(rb_ref[here, :], sb_ref[...], preferred_element_type=F32)
        inner = (25.0 / 16.0) * v_ref[here, :] - product
        factor = jnp.where(diagonal(part * step, step), 1.25, 0.0) - 0.25 * s_ref[here, :]
        wb_ref[here, :] = (quarter * ((5.0 * factor - inner) * 0.25)).astype(BF16)

    own_value, other_value = masked_rows(own[0], other[...], scalars[3], scalars[4])
    root = wb_ref[...]
    update_own[...] = jnp.dot(own_value, root, preferred_element_type=F32).astype(BF16)
    update_other[...] = jnp.dot(other_value, root, preferred_element_type=F32).astype(BF16)

    @pl.when(scalars[5] == block)
    def _():
        root_own[...] = wb_ref[...]

    @pl.when(scalars[6] == block)
    def _():
        root_other[...] = wb_ref[...]


def shifted(value, axis, distance):
    return lax.ppermute(value, axis, [(k, (k + distance) % SIDE) for k in range(SIDE)])


def swapped(value):
    return lax.ppermute(value, "core", [(0, 1), (1, 0)])


def body(gradients, row_counts, block_owner):
    z, x, core = (lax.axis_index(name).astype(jnp.int32) for name in ("z", "x", "core"))
    tp_index = lax.axis_index("tp")
    _, row_slots, columns = gradients.shape
    per_device = columns // BLOCK
    index = (z * SIDE + x) * 2 + core
    partner = index + 1 - 2 * core
    total_rows = jnp.sum(row_counts).astype(F32)
    inverse_rows = (1.0 / total_rows).reshape(1)
    local_owner = lax.dynamic_slice(block_owner, (core, tp_index * per_device), (1, per_device))[0]
    position = jnp.arange(per_device, dtype=jnp.int32)
    mine = jnp.max(jnp.where(local_owner == index, position, -1))
    theirs = jnp.max(jnp.where(local_owner == partner, position, -1))
    scalars = jnp.stack(
        [core, z, x, row_counts[index], row_counts[partner], mine, theirs]
    ).astype(jnp.int32)

    away = jnp.where(core == 0, gradients[1], gradients[0])
    other = swapped(away)

    chunk4 = (SIDE, HALF, WIDE)
    chunk1 = (HALF, WIDE)
    in_vmem = pl.BlockSpec(memory_space=pltpu.VMEM)
    packed = pl.pallas_call(
        gram_kernel,
        grid_spec=pltpu.PrefetchScalarGridSpec(
            num_scalar_prefetch=1,
            grid=(1,),
            in_specs=[
                pl.BlockSpec((1, row_slots, columns), lambda i, s: (s[0], 0, 0)),
                pl.BlockSpec((row_slots, columns), lambda i, s: (0, 0)),
            ],
            out_specs=[pl.BlockSpec(chunk4, lambda i, s: (0, 0, 0))] * 8,
            scratch_shapes=[
                pltpu.VMEM((2 * row_slots, BLOCK + BLOCK // 2), BF16),
                pltpu.VMEM((16, HALF, WIDE), F32),
            ],
        ),
        out_shape=[jax.ShapeDtypeStruct(chunk4, F32 if k % 4 == 0 else BF16) for k in range(8)],
        compiler_params=VMEM,
        name="gram",
    )(scalars, gradients, other)

    axes = ("x", "z")
    received = list(packed)
    for side in range(2):
        for k in range(1, SIDE):
            received[4 * side + k] = shifted(packed[4 * side + k], axes[side], k)
    summed = pl.pallas_call(
        first_sum_kernel,
        in_specs=[in_vmem] * 8,
        out_specs=[in_vmem] * 8,
        out_shape=[jax.ShapeDtypeStruct(chunk1, F32 if k % 4 == 0 else BF16) for k in range(8)],
        compiler_params=VMEM,
        name="first_sum",
    )(*received)
    received = list(summed)
    for side in range(2):
        for k in range(1, SIDE):
            received[4 * side + k] = shifted(summed[4 * side + k], axes[1 - side], k)
    reduced = pl.pallas_call(
        second_sum_kernel,
        in_specs=[in_vmem] * 8,
        out_specs=[in_vmem] * 2,
        out_shape=[jax.ShapeDtypeStruct(chunk1, BF16)] * 2,
        compiler_params=VMEM,
        name="second_sum",
    )(*received)
    sets = []
    for side in range(2):
        line = [reduced[side]]
        for k in range(1, SIDE):
            line.append(shifted(reduced[side], axes[1 - side], -k))
        line = jnp.stack(line)
        sets.append(line)
        for k in range(1, SIDE):
            sets.append(shifted(line, axes[side], -k))

    whole = pl.BlockSpec(chunk4, lambda k, s: (0, 0, 0))
    update_own, update_other, root_own, root_other = pl.pallas_call(
        root_kernel,
        grid_spec=pltpu.PrefetchScalarGridSpec(
            num_scalar_prefetch=1,
            grid=(per_device,),
            in_specs=[
                pl.BlockSpec(memory_space=pltpu.SMEM),
                pl.BlockSpec((1, row_slots, BLOCK), lambda k, s: (s[0], 0, k)),
                pl.BlockSpec((row_slots, BLOCK), lambda k, s: (0, k)),
            ]
            + [whole] * 8,
            out_specs=[
                pl.BlockSpec((row_slots, BLOCK), lambda k, s: (0, k)),
                pl.BlockSpec((row_slots, BLOCK), lambda k, s: (0, k)),
                pl.BlockSpec((BLOCK, BLOCK), lambda k, s: (0, 0)),
                pl.BlockSpec((BLOCK, BLOCK), lambda k, s: (0, 0)),
            ],
            scratch_shapes=[pltpu.VMEM((BLOCK, BLOCK), F32)] * 3
            + [pltpu.VMEM((BLOCK, BLOCK), BF16)] * 3,
        ),
        out_shape=[
            jax.ShapeDtypeStruct((row_slots, columns), BF16),
            jax.ShapeDtypeStruct((row_slots, columns), BF16),
            jax.ShapeDtypeStruct((BLOCK, BLOCK), BF16),
            jax.ShapeDtypeStruct((BLOCK, BLOCK), BF16),
        ],
        compiler_params=VMEM,
        name="root",
    )(scalars, inverse_rows, gradients, other, *sets)

    update_back = swapped(update_other)
    root_back = swapped(root_other)
    update = jnp.stack(
        [
            jnp.where(core == 0, update_own, update_back),
            jnp.where(core == 0, update_back, update_own),
        ]
    )
    owned = jnp.where(mine >= 0, root_own, root_back)
    return update, owned


def solution(mesh):
    cores = Mesh(mesh.devices.reshape(SIDE, SIDE, 2, SIDE), ("z", "x", "core", "tp"))
    rows = ("z", "x", "core")
    return jax.shard_map(
        body,
        mesh=cores,
        in_specs=(P(None, rows, "tp"), P(), P()),
        out_specs=(P(None, rows, "tp"), P(rows, "tp")),
        check_vma=False,
    )
```

time: 446 us -> 137 us (0.31)
  waiting for transfers between devices: 293 us -> 45.4 us
  matrix products: 83.6 us -> 0 us
  Pallas kernels: 0 us -> 35.1 us
  starting transfers between devices: 0.08 us -> 35 us
  other arithmetic: 33.1 us -> 9.32 us
  between operations: 18.1 us -> 2.22 us
  local copies, waits for them, and re-layouts: 13.3 us -> 7.74 us
    psum x2 -> x0, waiting for transfers between devices: 293 us -> none  [the longest x1 175 us: body(): summed = lax.psum(partial_value, 'fsdp')]
    dot_general x6 -> x0, matrix products: 83.6 us -> none  [the longest x1 19.5 us: newton_root(): jnp.dot(jnp.sqrt(jnp.sqrt(scaling)) * factor_one, factor_two, precision=l...]
    ppermute x0 -> x27, waiting for transfers between devices: none -> 45.4 us  [the longest x24 40.7 us: shifted(): lax.ppermute(value, axis, [(k, (k + distance) % SIDE) for k in range(SIDE)])]
    pallas_call x0 -> x4, Pallas kernels: none -> 35.1 us  [the longest x1 25 us: body(): pl.pallas_call(root_kernel, grid_spec=pltpu.PrefetchScalarGridSpec(num_sc...]
    ppermute x0 -> x27, starting transfers between devices: none -> 35 us  [the longest x24 34.3 us: shifted(): lax.ppermute(value, axis, [(k, (k + distance) % SIDE) for k in range(SIDE)])]
    reduce_sum x3 -> x1, other arithmetic: 11 us -> 0.63 us  [body(): total_rows = jnp.sum(row_counts).astype(F32)]
    another operation x2 -> x4, other arithmetic: 12.2 us -> 4.74 us  [the longest x2 2.87 us: body(): jnp.stack([jnp.where(core == 0, update_own, update_back), jnp.where(core...]
    add x1 -> x0, other arithmetic: 6.83 us -> none  [body(): statistic = summed / total_rows + damping * identity]
  transfers between devices with their start and end apart: 2 -> 27, of which waited for: 2 -> 15; matrix products, arithmetic and copies ran while one was open for 0% -> 7% of each run, Pallas kernels for 0% -> 0%
where the time goes in v1:
time: 137 us; the launch traced here: 135 us
  waiting for transfers between devices  45.4 us (33%)
  Pallas kernels  35.1 us (26%)
  starting transfers between devices  35 us (26%)
  other arithmetic  9.32 us (7%)
  local copies, waits for them, and re-layouts  7.74 us (6%)
  between operations  2.22 us (2%)
    ppermute x24, waiting for transfers between devices, shifted(): lax.ppermute(value, axis, [(k, (k + distance) % SIDE) for k in range(SIDE)])  40.7 us
    ppermute x24, starting transfers between devices, shifted(): lax.ppermute(value, axis, [(k, (k + distance) % SIDE) for k in range(SIDE)])  34.3 us
    pallas_call x1, Pallas kernels, body(): pl.pallas_call(root_kernel, grid_spec=pltpu.PrefetchScalarGridSpec(num_sc...  25 us
    pallas_call x1, Pallas kernels, body(): pl.pallas_call(gram_kernel, grid_spec=pltpu.PrefetchScalarGridSpec(num_sc...  5.37 us
    ppermute x3, waiting for transfers between devices, swapped(): return lax.ppermute(value, 'core', [(0, 1), (1, 0)])  4.72 us
    unnamed x48, local copies, waits for them, and re-layouts  3.98 us
    another operation x1, local copies, waits for them, and re-layouts, body(): jnp.stack([core, z, x, row_counts[index], row_counts[partner], mine, thei...  3.11 us
    another operation x2, other arithmetic, body(): jnp.stack([jnp.where(core == 0, update_own, update_back), jnp.where(core...  2.87 us
  transfers between devices with their start and end apart: 27, of which 15 were waited for; matrix products, arithmetic and copies ran while one was open for 7% of the time, Pallas kernels for 0%

profile of v1, /device:TPU:6, one launch (start us, length us, event | category | flops | bytes accessed | tf_op | source)
XLA Modules:
  0.0 134.8 jit_solution(212872200738776162)
XLA Ops:
  0.7 1.7 %select_bitcast_fusion.2 = bf16[256,2048]{1,0:T(8,128)(2,1)S(1)} fusion(bf16[2,256,2048]{2,1,0:T(8,128)(2,1)} %own.3, pred[]{:T(512)S(6)} %eq.23), kind=kLoop, calls=%fused_computation.4 | loop fusion | flops 524288 | bytes 3145729 | tf_op jit(solution)/shard_map/jit(_where)/select_n | solution.py:201
  3.1 0.8 fusion.1
  3.9 3.1 %stack.62.scalars = s32[7]{0:T(128)} concatenate(s32[1]{0:T(128)} %bitcast, s32[1]{0:T(128)} %bitcast.1, s32[1]{0:T(128)} %bitcast.2, s32[1]{0:T(128)} %get-tuple-element.51, s32[1]{0:T(128)} %get-tuple-element.50, s32[1]{0:T(128)} %bitcast.4, s32[1]{0:T(128)} %bitcast.6), dimensions={0} | concatenate | bytes 56 | tf_op jit(solution)/shard_map/stack | solution.py:197
  7.0 1.0 copy-done
  7.9 5.4 %gram.1 = (f32[4,64,640]{2,1,0:T(8,128)}, bf16[4,64,640]{2,1,0:T(8,128)(2,1)}, bf16[4,64,640]{2,1,0:T(8,128)(2,1)}, bf16[4,64,640]{2,1,0:T(8,128)(2,1)}, f32[4,6...) custom-call(s32[7]{0:T(128)} %stack.62.scalars, ...), custom_call_target="tpu_custom_call" | custom-call | tf_op jit(solution)/shard_map/gram/pallas_call | solution.py:207
  13.7 2.5 %collective-permute-start.2 = (bf16[4,64,640]{2,1,0:T(8,128)(2,1)}, bf16[4,64,640]{2,1,0:T(8,128)(2,1)S(1)}, u32[]{:S(2)}, u32[]{:S(2)}) collective-permute-start(bf16[4,64,640]{2,1,0:T(8,128)(2,1)} %get-tuple-element.26), channel_id=1, source_target_pairs={{0,16},{8,24},{16,0},{24,8},{1,17},{9,25},{17,1},{25,9},{2,18},{10... | collective-permute-start | bytes 983048 | tf_op jit(solution)/shard_map/ppermute | solution.py:177
  16.2 1.9 %collective-permute-start.4 = (bf16[4,64,640]{2,1,0:T(8,128)(2,1)}, bf16[4,64,640]{2,1,0:T(8,128)(2,1)S(1)}, u32[]{:S(2)}, u32[]{:S(2)}) collective-permute-start(bf16[4,64,640]{2,1,0:T(8,128)(2,1)} %get-tuple-element.29), channel_id=1, source_target_pairs={{0,32},{32,64},{64,96},{96,0},{1,33},{33,65},{65,97},{97,1},{2,34}... | collective-permute-start | bytes 983048 | tf_op jit(solution)/shard_map/ppermute | solution.py:177
  18.1 3.6 %collective-permute-start.5 = (bf16[4,64,640]{2,1,0:T(8,128)(2,1)}, bf16[4,64,640]{2,1,0:T(8,128)(2,1)S(1)}, u32[]{:S(2)}, u32[]{:S(2)}) collective-permute-start(bf16[4,64,640]{2,1,0:T(8,128)(2,1)} %get-tuple-element.30), channel_id=1, source_target_pairs={{0,64},{32,96},{64,0},{96,32},{1,65},{33,97},{65,1},{97,33},{2,66}... | collective-permute-start | bytes 983048 | tf_op jit(solution)/shard_map/ppermute | solution.py:177
  21.7 2.4 %collective-permute-done.1.refs_1_ = bf16[4,64,640]{2,1,0:T(8,128)(2,1)S(1)} collective-permute-done((bf16[4,64,640]{2,1,0:T(8,128)(2,1)}, bf16[4,64,640]{2,1,0:T(8,128)(2,1)S(1)}, u32[]{:S(2)}, u32[]{:S(2)}) %collective-permute-start.1) | collective-permute-done | bytes 327712 | tf_op jit(solution)/shard_map/ppermute | solution.py:177
  24.1 4.0 %collective-permute-start.6 = (bf16[4,64,640]{2,1,0:T(8,128)(2,1)}, bf16[4,64,640]{2,1,0:T(8,128)(2,1)S(1)}, u32[]{:S(2)}, u32[]{:S(2)}) collective-permute-start(bf16[4,64,640]{2,1,0:T(8,128)(2,1)} %get-tuple-element.31), channel_id=1, source_target_pairs={{0,96},{32,0},{64,32},{96,64},{1,97},{33,1},{65,33},{97,65},{2,98}... | collective-permute-start | bytes 983048 | tf_op jit(solution)/shard_map/ppermute | solution.py:177
  28.2 4.1 %collective-permute-done.3.refs_3_ = bf16[4,64,640]{2,1,0:T(8,128)(2,1)S(1)} collective-permute-done((bf16[4,64,640]{2,1,0:T(8,128)(2,1)}, bf16[4,64,640]{2,1,0:T(8,128)(2,1)S(1)}, u32[]{:S(2)}, u32[]{:S(2)}) %collective-permute-start.3) | collective-permute-done | bytes 327712 | tf_op jit(solution)/shard_map/ppermute | solution.py:177
  32.2 4.2 %collective-permute-done.5.refs_6_ = bf16[4,64,640]{2,1,0:T(8,128)(2,1)S(1)} collective-permute-done((bf16[4,64,640]{2,1,0:T(8,128)(2,1)}, bf16[4,64,640]{2,1,0:T(8,128)(2,1)S(1)}, u32[]{:S(2)}, u32[]{:S(2)}) %collective-permute-start.5) | collective-permute-done | bytes 327712 | tf_op jit(solution)/shard_map/ppermute | solution.py:177
  36.5 0.7 copy-done.14
  37.3 2.8 %first_sum.1 = (f32[64,640]{1,0:T(8,128)}, bf16[64,640]{1,0:T(8,128)(2,1)}, bf16[64,640]{1,0:T(8,128)(2,1)}, bf16[64,640]{1,0:T(8,128)(2,1)}, f32[64,640]{1,0:T(...) custom-call(f32[4,64,640]{2,1,0:T(8,128)} %get-tuple-element.24.refs_0_, ...), custom_call_target="tpu_custom_call" | custom-call | tf_op jit(solution)/shard_map/first_sum/pallas_call | solution.py:232
  40.1 1.5 %collective-permute-start.7 = (bf16[64,640]{1,0:T(8,128)(2,1)}, bf16[64,640]{1,0:T(8,128)(2,1)S(1)}, u32[]{:S(2)}, u32[]{:S(2)}) collective-permute-start(bf16[64,640]{1,0:T(8,128)(2,1)} %get-tuple-element.33), channel_id=1, source_target_pairs={{0,32},{32,64},{64,96},{96,0},{1,33},{33,65},{65,97},{97,1},{2,34}... | collective-permute-start | bytes 245768 | tf_op jit(solution)/shard_map/ppermute | solution.py:177
  41.6 2.4 %collective-permute-start.8 = (bf16[64,640]{1,0:T(8,128)(2,1)}, bf16[64,640]{1,0:T(8,128)(2,1)S(1)}, u32[]{:S(2)}, u32[]{:S(2)}) collective-permute-start(bf16[64,640]{1,0:T(8,128)(2,1)} %get-tuple-element.34), channel_id=1, source_target_pairs={{0,64},{32,96},{64,0},{96,32},{1,65},{33,97},{65,1},{97,33},{2,66}... | collective-permute-start | bytes 245768 | tf_op jit(solution)/shard_map/ppermute | solution.py:177
  44.0 0.9 collective-permute-start.9
  44.8 3.0 %collective-permute-start.10 = (bf16[64,640]{1,0:T(8,128)(2,1)}, bf16[64,640]{1,0:T(8,128)(2,1)S(1)}, u32[]{:S(2)}, u32[]{:S(2)}) collective-permute-start(bf16[64,640]{1,0:T(8,128)(2,1)} %get-tuple-element.37), channel_id=1, source_target_pairs={{0,8},{8,16},{16,24},{24,0},{1,9},{9,17},{17,25},{25,1},{2,10},{10... | collective-permute-start | bytes 245768 | tf_op jit(solution)/shard_map/ppermute | solution.py:177
  47.9 1.4 %collective-permute-start.12 = (bf16[64,640]{1,0:T(8,128)(2,1)}, bf16[64,640]{1,0:T(8,128)(2,1)S(1)}, u32[]{:S(2)}, u32[]{:S(2)}) collective-permute-start(bf16[64,640]{1,0:T(8,128)(2,1)} %get-tuple-element.39), channel_id=1, source_target_pairs={{0,24},{8,0},{16,8},{24,16},{1,25},{9,1},{17,9},{25,17},{2,26},{10... | collective-permute-start | bytes 245768 | tf_op jit(solution)/shard_map/ppermute | solution.py:177
  49.3 1.0 collective-permute-done.10.refs_5_
  50.3 3.8 %collective-permute-done.11.refs_6_ = bf16[64,640]{1,0:T(8,128)(2,1)S(1)} collective-permute-done((bf16[64,640]{1,0:T(8,128)(2,1)}, bf16[64,640]{1,0:T(8,128)(2,1)S(1)}, u32[]{:S(2)}, u32[]{:S(2)}) %collective-permute-start.11) | collective-permute-done | bytes 81952 | tf_op jit(solution)/shard_map/ppermute | solution.py:177
  55.3 2.0 %second_sum.1 = (bf16[64,640]{1,0:T(8,128)(2,1)}, bf16[64,640]{1,0:T(8,128)(2,1)}) custom-call(f32[64,640]{1,0:T(8,128)} %get-tuple-element.32.refs_0_, bf16[64,640]{1,0:T(8,128)(2,1)} %copy-done.16, bf16[64,640]{1,0:T(8,128)(2,1)} %copy-done.17, bf16[64,640]{1,0:T(8,128)(2,1)} %copy-done.18, f32[64,640]{1,0:T(8,128)} %get-tuple-element.36.refs_4_, ...), custom_call_target="tpu_custom_call" | custom-call | tf_op jit(solution)/shard_map/second_sum/pallas_call | solution.py:244
  57.2 0.8 collective-permute-start.21
  58.6 1.4 %collective-permute-start.19 = (bf16[64,640]{1,0:T(8,128)(2,1)}, bf16[64,640]{1,0:T(8,128)(2,1)S(1)}, u32[]{:S(2)}, u32[]{:S(2)}) collective-permute-start(bf16[64,640]{1,0:T(8,128)(2,1)} %get-tuple-element.41), channel_id=1, source_target_pairs={{0,24},{8,0},{16,8},{24,16},{1,25},{9,1},{17,9},{25,17},{2,26},{10... | collective-permute-start | bytes 245768 | tf_op jit(solution)/shard_map/ppermute | solution.py:177
  60.0 1.9 %collective-permute-done.21 = bf16[64,640]{1,0:T(8,128)(2,1)S(1)} collective-permute-done((bf16[64,640]{1,0:T(8,128)(2,1)}, bf16[64,640]{1,0:T(8,128)(2,1)S(1)}, u32[]{:S(2)}, u32[]{:S(2)}) %collective-permute-start.21) | collective-permute-done | bytes 81952 | tf_op jit(solution)/shard_map/ppermute | solution.py:177
  61.9 2.3 %collective-permute-done.20 = bf16[64,640]{1,0:T(8,128)(2,1)S(1)} collective-permute-done((bf16[64,640]{1,0:T(8,128)(2,1)}, bf16[64,640]{1,0:T(8,128)(2,1)S(1)}, u32[]{:S(2)}, u32[]{:S(2)}) %collective-permute-start.20) | collective-permute-done | bytes 81952 | tf_op jit(solution)/shard_map/ppermute | solution.py:177
  64.2 0.8 collective-permute-done.19
  65.1 0.9 pad_maximum_fusion.2.refs_4_
  66.0 0.8 collective-permute-start.24
  66.8 0.7 collective-permute-start.15
  67.4 3.3 %collective-permute-start.14 = (bf16[64,640]{1,0:T(8,128)(2,1)}, bf16[64,640]{1,0:T(8,128)(2,1)S(1)}, u32[]{:S(2)}, u32[]{:S(2)}) collective-permute-start(bf16[64,640]{1,0:T(8,128)(2,1)} %get-tuple-element.40), channel_id=1, source_target_pairs={{0,64},{32,96},{64,0},{96,32},{1,65},{33,97},{65,1},{97,33},{2,66}... | collective-permute-start | bytes 245768 | tf_op jit(solution)/shard_map/ppermute | solution.py:177
  71.0 1.9 %collective-permute-start.23 = (bf16[4,64,640]{2,1,0:T(8,128)(2,1)S(1)}, bf16[4,64,640]{2,1,0:T(8,128)(2,1)S(1)}, u32[]{:S(2)}, u32[]{:S(2)}) collective-permute-start(bf16[4,64,640]{2,1,0:T(8,128)(2,1)S(1)} %pad_maximum_fusion.2.refs_4_), channel_id=1, source_target_pairs={{0,64},{32,96},{64,0},{96,32},{1,65},{33,97},{65,1},{97,33},{2,66}... | collective-permute-start | bytes 983048 | tf_op jit(solution)/shard_map/ppermute | solution.py:177
  72.9 10.9 %collective-permute-done.15 = bf16[64,640]{1,0:T(8,128)(2,1)S(1)} collective-permute-done((bf16[64,640]{1,0:T(8,128)(2,1)}, bf16[64,640]{1,0:T(8,128)(2,1)S(1)}, u32[]{:S(2)}, u32[]{:S(2)}) %collective-permute-start.15) | collective-permute-done | bytes 81952 | tf_op jit(solution)/shard_map/ppermute | solution.py:177
  83.8 0.9 pad_maximum_fusion.1.refs_0_
  84.8 1.0 collective-permute-start.18
  85.8 1.3 collective-permute-start.17
  87.1 0.7 collective-permute-start.16
  89.1 1.8 %collective-permute-done.22.refs_5_ = bf16[4,64,640]{2,1,0:T(8,128)(2,1)S(1)} collective-permute-done((bf16[4,64,640]{2,1,0:T(8,128)(2,1)S(1)}, bf16[4,64,640]{2,1,0:T(8,128)(2,1)S(1)}, u32[]{:S(2)}, u32[]{:S(2)}) %collective-permute-start.22) | collective-permute-done | bytes 327712 | tf_op jit(solution)/shard_map/ppermute | solution.py:177
  90.9 1.0 collective-permute-done.18.refs_3_
  91.9 2.6 %collective-permute-done.17.refs_2_ = bf16[4,64,640]{2,1,0:T(8,128)(2,1)S(1)} collective-permute-done((bf16[4,64,640]{2,1,0:T(8,128)(2,1)S(1)}, bf16[4,64,640]{2,1,0:T(8,128)(2,1)S(1)}, u32[]{:S(2)}, u32[]{:S(2)}) %collective-permute-start.17) | collective-permute-done | bytes 327712 | tf_op jit(solution)/shard_map/ppermute | solution.py:177
  94.5 3.4 %collective-permute-done.16.refs_1_ = bf16[4,64,640]{2,1,0:T(8,128)(2,1)S(1)} collective-permute-done((bf16[4,64,640]{2,1,0:T(8,128)(2,1)S(1)}, bf16[4,64,640]{2,1,0:T(8,128)(2,1)S(1)}, u32[]{:S(2)}, u32[]{:S(2)}) %collective-permute-start.16) | collective-permute-done | bytes 327712 | tf_op jit(solution)/shard_map/ppermute | solution.py:177
  97.9 0.7 copy-done.9
  98.6 25.0 %root.1 = (bf16[256,2048]{1,0:T(8,128)(2,1)}, bf16[256,2048]{1,0:T(8,128)(2,1)}, bf16[1024,1024]{1,0:T(8,128)(2,1)}, bf16[1024,1024]{1,0:T(8,128)(2,1)}) custom-call(s32[7]{0:T(128)} %stack.62.scalars, f32[1]{0:T(128)} %bitcast.7.inverse_rows, bf16[2,256,2048]{2,1,0:T(8,128)(2,1)} %own.3, bf16[256,2048]{1,0:T(8,128)(2,1)} %copy-done, ...), custom_call_target="tpu_custom_call" | custom-call | tf_op jit(solution)/shard_map/root/pallas_call | solution.py:263
  124.8 4.7 %collective-permute-done.25 = bf16[256,2048]{1,0:T(8,128)(2,1)S(1)} collective-permute-done((bf16[256,2048]{1,0:T(8,128)(2,1)}, bf16[256,2048]{1,0:T(8,128)(2,1)S(1)}, u32[]{:S(2)}, u32[]{:S(2)}) %collective-permute-start.25) | collective-permute-done | bytes 1048608 | tf_op jit(solution)/shard_map/ppermute | solution.py:181
  129.6 1.4 %select_bitcast_fusion.1 = (bf16[1,256,2048]{2,1,0:T(8,128)(2,1)S(1)}, bf16[1,256,2048]{2,1,0:T(8,128)(2,1)S(1)}) fusion(bf16[256,2048]{1,0:T(8,128)(2,1)} %get-tuple-element.42, bf16[256,2048]{1,0:T(8,128)(2,1)S(1)} %collective-permute-done.25, pred[]{:T(512)S(6)} %eq.23), kind=kLoop, calls=%fused_computation.3 | loop fusion | flops 1048576 | bytes 4194305 | tf_op jit(solution)/shard_map/stack | solution.py:295
  130.9 1.5 %pad_maximum_fusion = bf16[2,256,2048]{2,1,0:T(8,128)(2,1)} fusion(bf16[1,256,2048]{2,1,0:T(8,128)(2,1)S(1)} %get-tuple-element.49, bf16[1,256,2048]{2,1,0:T(8,128)(2,1)S(1)} %get-tuple-element.48), kind=kLoop, calls=%fused_computation | loop fusion | flops 1048576 | bytes 4194304 | tf_op jit(solution)/shard_map/stack | solution.py:295
  132.4 0.8 copy-done.1
  133.3 1.5 %broadcast_select_fusion = bf16[1024,1024]{1,0:T(8,128)(2,1)} fusion(bf16[1024,1024]{1,0:T(8,128)(2,1)S(1)} %copy-done.1, bf16[1024,1024]{1,0:T(8,128)(2,1)S(1)} %collective-permute-done.26, pred[]{:T(512)S(6)} %ge.3), kind=kLoop, calls=%fused_computation.1 | loop fusion | flops 1048576 | bytes 6291457 | tf_op jit(solution)/shard_map/jit(_where)/select_n | solution.py:301
  (68 shorter events, 4.6 us)
Async XLA Ops:
  0.6 1.8 %copy-start.22 = (s32[32]{0:T(128)S(1)}, s32[32]{0:T(128)}, u32[]{:S(2)}) copy-start(s32[32]{0:T(128)} %param.4) | copy-start | bytes 388
  0.6 2.5 %copy-start.23 = (s32[2,8]{1,0:T(2,128)S(1)}, s32[2,8]{1,0:T(2,128)}, u32[]{:S(2)}) copy-start(s32[2,8]{1,0:T(2,128)} %param.5) | copy-start | bytes 196
  2.3 4.7 %collective-permute-start = (bf16[256,2048]{1,0:T(8,128)(2,1)S(1)}, bf16[256,2048]{1,0:T(8,128)(2,1)S(1)}, u32[]{:S(2)}, u32[]{:S(2)}) collective-permute-start(bf16[256,2048]{1,0:T(8,128)(2,1)S(1)} %select_bitcast_fusion.2), channel_id=1, source_target_pairs={{0,4},{4,0},{1,5},{5,1},{2,6},{6,2},{3,7},{7,3},{8,12},{12,8},{9,1... | collective-permute-start | bytes 3145736 | tf_op jit(solution)/shard_map/ppermute | solution.py:181
  7.0 1.0 copy-start
  13.3 10.8 %collective-permute-start.1 = (bf16[4,64,640]{2,1,0:T(8,128)(2,1)}, bf16[4,64,640]{2,1,0:T(8,128)(2,1)S(1)}, u32[]{:S(2)}, u32[]{:S(2)}) collective-permute-start(bf16[4,64,640]{2,1,0:T(8,128)(2,1)} %get-tuple-element.25), channel_id=1, source_target_pairs={{0,8},{8,16},{16,24},{24,0},{1,9},{9,17},{17,25},{25,1},{2,10},{10... | collective-permute-start | bytes 983048 | tf_op jit(solution)/shard_map/ppermute | solution.py:177
  13.7 14.5 %collective-permute-start.2 = (bf16[4,64,640]{2,1,0:T(8,128)(2,1)}, bf16[4,64,640]{2,1,0:T(8,128)(2,1)S(1)}, u32[]{:S(2)}, u32[]{:S(2)}) collective-permute-start(bf16[4,64,640]{2,1,0:T(8,128)(2,1)} %get-tuple-element.26), channel_id=1, source_target_pairs={{0,16},{8,24},{16,0},{24,8},{1,17},{9,25},{17,1},{25,9},{2,18},{10... | collective-permute-start | bytes 983048 | tf_op jit(solution)/shard_map/ppermute | solution.py:177
  16.2 16.0 %collective-permute-start.3 = (bf16[4,64,640]{2,1,0:T(8,128)(2,1)}, bf16[4,64,640]{2,1,0:T(8,128)(2,1)S(1)}, u32[]{:S(2)}, u32[]{:S(2)}) collective-permute-start(bf16[4,64,640]{2,1,0:T(8,128)(2,1)} %get-tuple-element.27), channel_id=1, source_target_pairs={{0,24},{8,0},{16,8},{24,16},{1,25},{9,1},{17,9},{25,17},{2,26},{10... | collective-permute-start | bytes 983048 | tf_op jit(solution)/shard_map/ppermute | solution.py:177
  16.2 16.0 %collective-permute-start.4 = (bf16[4,64,640]{2,1,0:T(8,128)(2,1)}, bf16[4,64,640]{2,1,0:T(8,128)(2,1)S(1)}, u32[]{:S(2)}, u32[]{:S(2)}) collective-permute-start(bf16[4,64,640]{2,1,0:T(8,128)(2,1)} %get-tuple-element.29), channel_id=1, source_target_pairs={{0,32},{32,64},{64,96},{96,0},{1,33},{33,65},{65,97},{97,1},{2,34}... | collective-permute-start | bytes 983048 | tf_op jit(solution)/shard_map/ppermute | solution.py:177
  18.1 18.3 %collective-permute-start.5 = (bf16[4,64,640]{2,1,0:T(8,128)(2,1)}, bf16[4,64,640]{2,1,0:T(8,128)(2,1)S(1)}, u32[]{:S(2)}, u32[]{:S(2)}) collective-permute-start(bf16[4,64,640]{2,1,0:T(8,128)(2,1)} %get-tuple-element.30), channel_id=1, source_target_pairs={{0,64},{32,96},{64,0},{96,32},{1,65},{33,97},{65,1},{97,33},{2,66}... | collective-permute-start | bytes 983048 | tf_op jit(solution)/shard_map/ppermute | solution.py:177
  24.1 12.3 %copy-start.10 = (bf16[4,64,640]{2,1,0:T(8,128)(2,1)}, bf16[4,64,640]{2,1,0:T(8,128)(2,1)S(1)}, u32[]{:S(2)}) copy-start(bf16[4,64,640]{2,1,0:T(8,128)(2,1)S(1)} %collective-permute-done.1.refs_1_) | copy-start | bytes 983044
  24.1 12.3 %collective-permute-start.6 = (bf16[4,64,640]{2,1,0:T(8,128)(2,1)}, bf16[4,64,640]{2,1,0:T(8,128)(2,1)S(1)}, u32[]{:S(2)}, u32[]{:S(2)}) collective-permute-start(bf16[4,64,640]{2,1,0:T(8,128)(2,1)} %get-tuple-element.31), channel_id=1, source_target_pairs={{0,96},{32,0},{64,32},{96,64},{1,97},{33,1},{65,33},{97,65},{2,98}... | collective-permute-start | bytes 983048 | tf_op jit(solution)/shard_map/ppermute | solution.py:177
  28.2 8.3 %copy-start.11 = (bf16[4,64,640]{2,1,0:T(8,128)(2,1)}, bf16[4,64,640]{2,1,0:T(8,128)(2,1)S(1)}, u32[]{:S(2)}) copy-start(bf16[4,64,640]{2,1,0:T(8,128)(2,1)S(1)} %collective-permute-done.2.refs_2_) | copy-start | bytes 983044
  32.2 4.2 %copy-start.12 = (bf16[4,64,640]{2,1,0:T(8,128)(2,1)}, bf16[4,64,640]{2,1,0:T(8,128)(2,1)S(1)}, u32[]{:S(2)}) copy-start(bf16[4,64,640]{2,1,0:T(8,128)(2,1)S(1)} %collective-permute-done.3.refs_3_) | copy-start | bytes 983044
  32.2 4.3 %copy-start.13 = (bf16[4,64,640]{2,1,0:T(8,128)(2,1)}, bf16[4,64,640]{2,1,0:T(8,128)(2,1)S(1)}, u32[]{:S(2)}) copy-start(bf16[4,64,640]{2,1,0:T(8,128)(2,1)S(1)} %collective-permute-done.4.refs_5_) | copy-start | bytes 983044
  36.4 0.8 copy-start.15
  40.1 7.7 %collective-permute-start.7 = (bf16[64,640]{1,0:T(8,128)(2,1)}, bf16[64,640]{1,0:T(8,128)(2,1)S(1)}, u32[]{:S(2)}, u32[]{:S(2)}) collective-permute-start(bf16[64,640]{1,0:T(8,128)(2,1)} %get-tuple-element.33), channel_id=1, source_target_pairs={{0,32},{32,64},{64,96},{96,0},{1,33},{33,65},{65,97},{97,1},{2,34}... | collective-permute-start | bytes 245768 | tf_op jit(solution)/shard_map/ppermute | solution.py:177
  41.6 7.7 %collective-permute-start.8 = (bf16[64,640]{1,0:T(8,128)(2,1)}, bf16[64,640]{1,0:T(8,128)(2,1)S(1)}, u32[]{:S(2)}, u32[]{:S(2)}) collective-permute-start(bf16[64,640]{1,0:T(8,128)(2,1)} %get-tuple-element.34), channel_id=1, source_target_pairs={{0,64},{32,96},{64,0},{96,32},{1,65},{33,97},{65,1},{97,33},{2,66}... | collective-permute-start | bytes 245768 | tf_op jit(solution)/shard_map/ppermute | solution.py:177
  44.0 5.3 %collective-permute-start.9 = (bf16[64,640]{1,0:T(8,128)(2,1)}, bf16[64,640]{1,0:T(8,128)(2,1)S(1)}, u32[]{:S(2)}, u32[]{:S(2)}) collective-permute-start(bf16[64,640]{1,0:T(8,128)(2,1)} %get-tuple-element.35), channel_id=1, source_target_pairs={{0,96},{32,0},{64,32},{96,64},{1,97},{33,1},{65,33},{97,65},{2,98}... | collective-permute-start | bytes 245768 | tf_op jit(solution)/shard_map/ppermute | solution.py:177
  44.8 5.5 %collective-permute-start.10 = (bf16[64,640]{1,0:T(8,128)(2,1)}, bf16[64,640]{1,0:T(8,128)(2,1)S(1)}, u32[]{:S(2)}, u32[]{:S(2)}) collective-permute-start(bf16[64,640]{1,0:T(8,128)(2,1)} %get-tuple-element.37), channel_id=1, source_target_pairs={{0,8},{8,16},{16,24},{24,0},{1,9},{9,17},{17,25},{25,1},{2,10},{10... | collective-permute-start | bytes 245768 | tf_op jit(solution)/shard_map/ppermute | solution.py:177
  47.8 6.3 %collective-permute-start.11 = (bf16[64,640]{1,0:T(8,128)(2,1)}, bf16[64,640]{1,0:T(8,128)(2,1)S(1)}, u32[]{:S(2)}, u32[]{:S(2)}) collective-permute-start(bf16[64,640]{1,0:T(8,128)(2,1)} %get-tuple-element.38), channel_id=1, source_target_pairs={{0,16},{8,24},{16,0},{24,8},{1,17},{9,25},{17,1},{25,9},{2,18},{10... | collective-permute-start | bytes 245768 | tf_op jit(solution)/shard_map/ppermute | solution.py:177
  47.9 6.8 %copy-start.16 = (bf16[64,640]{1,0:T(8,128)(2,1)}, bf16[64,640]{1,0:T(8,128)(2,1)S(1)}, u32[]{:S(2)}) copy-start(bf16[64,640]{1,0:T(8,128)(2,1)S(1)} %collective-permute-done.7.refs_1_) | copy-start | bytes 245764
  47.9 6.8 %collective-permute-start.12 = (bf16[64,640]{1,0:T(8,128)(2,1)}, bf16[64,640]{1,0:T(8,128)(2,1)S(1)}, u32[]{:S(2)}, u32[]{:S(2)}) collective-permute-start(bf16[64,640]{1,0:T(8,128)(2,1)} %get-tuple-element.39), channel_id=1, source_target_pairs={{0,24},{8,0},{16,8},{24,16},{1,25},{9,1},{17,9},{25,17},{2,26},{10... | collective-permute-start | bytes 245768 | tf_op jit(solution)/shard_map/ppermute | solution.py:177
  49.3 5.4 %copy-start.17 = (bf16[64,640]{1,0:T(8,128)(2,1)}, bf16[64,640]{1,0:T(8,128)(2,1)S(1)}, u32[]{:S(2)}) copy-start(bf16[64,640]{1,0:T(8,128)(2,1)S(1)} %collective-permute-done.8.refs_2_) | copy-start | bytes 245764
  49.3 5.4 %copy-start.18 = (bf16[64,640]{1,0:T(8,128)(2,1)}, bf16[64,640]{1,0:T(8,128)(2,1)S(1)}, u32[]{:S(2)}) copy-start(bf16[64,640]{1,0:T(8,128)(2,1)S(1)} %collective-permute-done.9.refs_3_) | copy-start | bytes 245764
  50.3 4.4 %copy-start.19 = (bf16[64,640]{1,0:T(8,128)(2,1)}, bf16[64,640]{1,0:T(8,128)(2,1)S(1)}, u32[]{:S(2)}) copy-start(bf16[64,640]{1,0:T(8,128)(2,1)S(1)} %collective-permute-done.10.refs_5_) | copy-start | bytes 245764
  57.2 4.7 %collective-permute-start.21 = (bf16[64,640]{1,0:T(8,128)(2,1)}, bf16[64,640]{1,0:T(8,128)(2,1)S(1)}, u32[]{:S(2)}, u32[]{:S(2)}) collective-permute-start(bf16[64,640]{1,0:T(8,128)(2,1)} %get-tuple-element.41), channel_id=1, source_target_pairs={{0,8},{8,16},{16,24},{24,0},{1,9},{9,17},{17,25},{25,1},{2,10},{10... | collective-permute-start | bytes 245768 | tf_op jit(solution)/shard_map/ppermute | solution.py:177
  58.0 6.2 %collective-permute-start.20 = (bf16[64,640]{1,0:T(8,128)(2,1)}, bf16[64,640]{1,0:T(8,128)(2,1)S(1)}, u32[]{:S(2)}, u32[]{:S(2)}) collective-permute-start(bf16[64,640]{1,0:T(8,128)(2,1)} %get-tuple-element.41), channel_id=1, source_target_pairs={{0,16},{8,24},{16,0},{24,8},{1,17},{9,25},{17,1},{25,9},{2,18},{10... | collective-permute-start | bytes 245768 | tf_op jit(solution)/shard_map/ppermute | solution.py:177
  58.6 6.4 %collective-permute-start.19 = (bf16[64,640]{1,0:T(8,128)(2,1)}, bf16[64,640]{1,0:T(8,128)(2,1)S(1)}, u32[]{:S(2)}, u32[]{:S(2)}) collective-permute-start(bf16[64,640]{1,0:T(8,128)(2,1)} %get-tuple-element.41), channel_id=1, source_target_pairs={{0,24},{8,0},{16,8},{24,16},{1,25},{9,1},{17,9},{25,17},{2,26},{10... | collective-permute-start | bytes 245768 | tf_op jit(solution)/shard_map/ppermute | solution.py:177
  66.0 31.9 %copy-start.2 = (bf16[4,64,640]{2,1,0:T(8,128)(2,1)}, bf16[4,64,640]{2,1,0:T(8,128)(2,1)S(1)}, u32[]{:S(2)}) copy-start(bf16[4,64,640]{2,1,0:T(8,128)(2,1)S(1)} %pad_maximum_fusion.2.refs_4_) | copy-start | bytes 983044
  66.0 21.1 %collective-permute-start.24 = (bf16[4,64,640]{2,1,0:T(8,128)(2,1)S(1)}, bf16[4,64,640]{2,1,0:T(8,128)(2,1)S(1)}, u32[]{:S(2)}, u32[]{:S(2)}) collective-permute-start(bf16[4,64,640]{2,1,0:T(8,128)(2,1)S(1)} %pad_maximum_fusion.2.refs_4_), channel_id=1, source_target_pairs={{0,32},{32,64},{64,96},{96,0},{1,33},{33,65},{65,97},{97,1},{2,34}... | collective-permute-start | bytes 983048 | tf_op jit(solution)/shard_map/ppermute | solution.py:177
  66.8 17.0 %collective-permute-start.15 = (bf16[64,640]{1,0:T(8,128)(2,1)}, bf16[64,640]{1,0:T(8,128)(2,1)S(1)}, u32[]{:S(2)}, u32[]{:S(2)}) collective-permute-start(bf16[64,640]{1,0:T(8,128)(2,1)} %get-tuple-element.40), channel_id=1, source_target_pairs={{0,32},{32,64},{64,96},{96,0},{1,33},{33,65},{65,97},{97,1},{2,34}... | collective-permute-start | bytes 245768 | tf_op jit(solution)/shard_map/ppermute | solution.py:177
  67.4 16.4 %collective-permute-start.14 = (bf16[64,640]{1,0:T(8,128)(2,1)}, bf16[64,640]{1,0:T(8,128)(2,1)S(1)}, u32[]{:S(2)}, u32[]{:S(2)}) collective-permute-start(bf16[64,640]{1,0:T(8,128)(2,1)} %get-tuple-element.40), channel_id=1, source_target_pairs={{0,64},{32,96},{64,0},{96,32},{1,65},{33,97},{65,1},{97,33},{2,66}... | collective-permute-start | bytes 245768 | tf_op jit(solution)/shard_map/ppermute | solution.py:177
  70.8 13.0 %collective-permute-start.13 = (bf16[64,640]{1,0:T(8,128)(2,1)}, bf16[64,640]{1,0:T(8,128)(2,1)S(1)}, u32[]{:S(2)}, u32[]{:S(2)}) collective-permute-start(bf16[64,640]{1,0:T(8,128)(2,1)} %get-tuple-element.40), channel_id=1, source_target_pairs={{0,96},{32,0},{64,32},{96,64},{1,97},{33,1},{65,33},{97,65},{2,98}... | collective-permute-start | bytes 245768 | tf_op jit(solution)/shard_map/ppermute | solution.py:177
  71.0 18.1 %collective-permute-start.23 = (bf16[4,64,640]{2,1,0:T(8,128)(2,1)S(1)}, bf16[4,64,640]{2,1,0:T(8,128)(2,1)S(1)}, u32[]{:S(2)}, u32[]{:S(2)}) collective-permute-start(bf16[4,64,640]{2,1,0:T(8,128)(2,1)S(1)} %pad_maximum_fusion.2.refs_4_), channel_id=1, source_target_pairs={{0,64},{32,96},{64,0},{96,32},{1,65},{33,97},{65,1},{97,33},{2,66}... | collective-permute-start | bytes 983048 | tf_op jit(solution)/shard_map/ppermute | solution.py:177
  83.8 7.1 %collective-permute-start.22 = (bf16[4,64,640]{2,1,0:T(8,128)(2,1)S(1)}, bf16[4,64,640]{2,1,0:T(8,128)(2,1)S(1)}, u32[]{:S(2)}, u32[]{:S(2)}) collective-permute-start(bf16[4,64,640]{2,1,0:T(8,128)(2,1)S(1)} %pad_maximum_fusion.2.refs_4_), channel_id=1, source_target_pairs={{0,96},{32,0},{64,32},{96,64},{1,97},{33,1},{65,33},{97,65},{2,98}... | collective-permute-start | bytes 983048 | tf_op jit(solution)/shard_map/ppermute | solution.py:177
  84.8 13.1 %copy-start.3 = (bf16[4,64,640]{2,1,0:T(8,128)(2,1)}, bf16[4,64,640]{2,1,0:T(8,128)(2,1)S(1)}, u32[]{:S(2)}) copy-start(bf16[4,64,640]{2,1,0:T(8,128)(2,1)S(1)} %pad_maximum_fusion.1.refs_0_) | copy-start | bytes 983044
  84.8 7.1 %collective-permute-start.18 = (bf16[4,64,640]{2,1,0:T(8,128)(2,1)S(1)}, bf16[4,64,640]{2,1,0:T(8,128)(2,1)S(1)}, u32[]{:S(2)}, u32[]{:S(2)}) collective-permute-start(bf16[4,64,640]{2,1,0:T(8,128)(2,1)S(1)} %pad_maximum_fusion.1.refs_0_), channel_id=1, source_target_pairs={{0,8},{8,16},{16,24},{24,0},{1,9},{9,17},{17,25},{25,1},{2,10},{10... | collective-permute-start | bytes 983048 | tf_op jit(solution)/shard_map/ppermute | solution.py:177
  85.8 8.7 %collective-permute-start.17 = (bf16[4,64,640]{2,1,0:T(8,128)(2,1)S(1)}, bf16[4,64,640]{2,1,0:T(8,128)(2,1)S(1)}, u32[]{:S(2)}, u32[]{:S(2)}) collective-permute-start(bf16[4,64,640]{2,1,0:T(8,128)(2,1)S(1)} %pad_maximum_fusion.1.refs_0_), channel_id=1, source_target_pairs={{0,16},{8,24},{16,0},{24,8},{1,17},{9,25},{17,1},{25,9},{2,18},{10... | collective-permute-start | bytes 983048 | tf_op jit(solution)/shard_map/ppermute | solution.py:177
  87.1 10.8 %copy-start.4 = (bf16[4,64,640]{2,1,0:T(8,128)(2,1)}, bf16[4,64,640]{2,1,0:T(8,128)(2,1)S(1)}, u32[]{:S(2)}) copy-start(bf16[4,64,640]{2,1,0:T(8,128)(2,1)S(1)} %collective-permute-done.24.refs_7_) | copy-start | bytes 983044
  87.1 10.8 %collective-permute-start.16 = (bf16[4,64,640]{2,1,0:T(8,128)(2,1)S(1)}, bf16[4,64,640]{2,1,0:T(8,128)(2,1)S(1)}, u32[]{:S(2)}, u32[]{:S(2)}) collective-permute-start(bf16[4,64,640]{2,1,0:T(8,128)(2,1)S(1)} %pad_maximum_fusion.1.refs_0_), channel_id=1, source_target_pairs={{0,24},{8,0},{16,8},{24,16},{1,25},{9,1},{17,9},{25,17},{2,26},{10... | collective-permute-start | bytes 983048 | tf_op jit(solution)/shard_map/ppermute | solution.py:177
  89.1 8.8 %copy-start.5 = (bf16[4,64,640]{2,1,0:T(8,128)(2,1)}, bf16[4,64,640]{2,1,0:T(8,128)(2,1)S(1)}, u32[]{:S(2)}) copy-start(bf16[4,64,640]{2,1,0:T(8,128)(2,1)S(1)} %collective-permute-done.23.refs_6_) | copy-start | bytes 983044
  90.9 7.0 %copy-start.6 = (bf16[4,64,640]{2,1,0:T(8,128)(2,1)}, bf16[4,64,640]{2,1,0:T(8,128)(2,1)S(1)}, u32[]{:S(2)}) copy-start(bf16[4,64,640]{2,1,0:T(8,128)(2,1)S(1)} %collective-permute-done.22.refs_5_) | copy-start | bytes 983044
  91.9 6.0 %copy-start.7 = (bf16[4,64,640]{2,1,0:T(8,128)(2,1)}, bf16[4,64,640]{2,1,0:T(8,128)(2,1)S(1)}, u32[]{:S(2)}) copy-start(bf16[4,64,640]{2,1,0:T(8,128)(2,1)S(1)} %collective-permute-done.18.refs_3_) | copy-start | bytes 983044
  94.5 3.5 %copy-start.8 = (bf16[4,64,640]{2,1,0:T(8,128)(2,1)}, bf16[4,64,640]{2,1,0:T(8,128)(2,1)S(1)}, u32[]{:S(2)}) copy-start(bf16[4,64,640]{2,1,0:T(8,128)(2,1)S(1)} %collective-permute-done.17.refs_2_) | copy-start | bytes 983044
  97.9 0.7 copy-start.9
  123.6 8.8 %collective-permute-start.26 = (bf16[1024,1024]{1,0:T(8,128)(2,1)}, bf16[1024,1024]{1,0:T(8,128)(2,1)S(1)}, u32[]{:S(2)}, u32[]{:S(2)}) collective-permute-start(bf16[1024,1024]{1,0:T(8,128)(2,1)} %get-tuple-element.45), channel_id=1, source_target_pairs={{0,4},{4,0},{1,5},{5,1},{2,6},{6,2},{3,7},{7,3},{8,12},{12,8},{9,1... | collective-permute-start | bytes 6291464 | tf_op jit(solution)/shard_map/ppermute | solution.py:181
  123.7 5.9 %collective-permute-start.25 = (bf16[256,2048]{1,0:T(8,128)(2,1)}, bf16[256,2048]{1,0:T(8,128)(2,1)S(1)}, u32[]{:S(2)}, u32[]{:S(2)}) collective-permute-start(bf16[256,2048]{1,0:T(8,128)(2,1)} %get-tuple-element.43), channel_id=1, source_target_pairs={{0,4},{4,0},{1,5},{5,1},{2,6},{6,2},{3,7},{7,3},{8,12},{12,8},{9,1... | collective-permute-start | bytes 3145736 | tf_op jit(solution)/shard_map/ppermute | solution.py:181
  130.9 2.4 %copy-start.1 = (bf16[1024,1024]{1,0:T(8,128)(2,1)S(1)}, bf16[1024,1024]{1,0:T(8,128)(2,1)}, u32[]{:S(2)}) copy-start(bf16[1024,1024]{1,0:T(8,128)(2,1)} %get-tuple-element.44) | copy-start | bytes 6291460
  (3 other events, 2.0 us)
